TPU v7x, 512 devices: a whole 4x4x16 slice. The times are simulated.
512 devices in a mesh: dp: 128 (over y, x, z_hi, core), mp: 4 (over z_lo).
Axes of the slice: x: 4, y: 4, z: 16 (z_hi: 4, z_lo: 4; z = z_hi * 4 + z_lo), core: 2. Of those that a mesh axis runs over, the one named last changes fastest.
Arguments:
- layer_input: bfloat16 [512, 8192], P('dp'), may hold values from -6 to 6
- pre_act: bfloat16 [512, 8192], P('dp', 'mp'), may hold values from -8 to 8
- hidden_adjoint: bfloat16 [512, 8192], P('dp', 'mp'), may hold values from -6 to 6
- output_adjoint: bfloat16 [512, 8192], P('dp', 'mp'), may hold values from -6 to 6
Outputs:
- precond_in: float32 [8192, 8192], P('dp', 'mp')
- direction_in: float32 [8192, 8192], P('dp', 'mp')
- precond_out: float32 [8192, 8192], P('dp', 'mp')
- direction_out: float32 [8192, 8192], P('dp', 'mp')
- sq_norm: float32 [], replicated
All inputs are finite; a program needn't handle non-finite values.
Results may differ from a plain program's by a relative error of at most 0.0029.
Values may be sent and summed in bfloat16 or wider, within the bound.
A program may use at most 64 MiB of HBM per device.

v0:
```python
import jax
import jax.numpy as jnp
from jax import lax
from jax.sharding import Mesh
from jax.sharding import PartitionSpec as P

D = 8192
H = 8192
DP = ("dp_0", "dp_1", "dp_2", "dp_3")
DP_MP = ("dp_0", "dp_1", "dp_2", "dp_3", "mp")


DAMPING = 0.1
EXPONENT = 0.75


def in_order(pieces, dim):
    pieces = jnp.moveaxis(pieces, 0, dim)
    lengths = pieces.shape
    return pieces.reshape(*lengths[:dim], lengths[dim] * lengths[dim + 1], *lengths[dim + 2 :])


def copy_for_each(x, axis):
    size = lax.axis_size(axis)
    return lax.all_to_all(jnp.broadcast_to(x[None], (size, *x.shape)), axis, 0, 0, tiled=True)


def gather_directly(x, axis, dim):
    return in_order(copy_for_each(x, axis), dim)


def split_up(x, dim, size):
    before, after = (x.shape[:dim], x.shape[dim + 1 :])
    return jnp.moveaxis(x.reshape(*before, size, -1, *after), dim, 0)


def exchange_in_order(pieces, axes, turns):
    lengths = [lax.axis_size(a) for a in axes]
    pieces = pieces.reshape(*lengths, *pieces.shape[1:])
    for k in turns:
        pieces = lax.all_to_all(pieces, axes[k], split_axis=k, concat_axis=k, tiled=True)
    return pieces.reshape(-1, *pieces.shape[len(axes) :])


def two_step_exchange(x, groups, turns, split_dim, concat_dim):
    size = lax.axis_size(groups[0]) * lax.axis_size(groups[1])
    pieces = split_up(x, split_dim, size)
    return in_order(exchange_in_order(pieces, groups, turns), concat_dim)


def side_by_side(arrays, axis, dim, along):
    ends, at = ([], 0)
    for a in arrays[:-1]:
        at += a.shape[along]
        ends.append(at)
    both = jnp.concatenate(arrays, axis=along)
    return tuple(jnp.split(lax.all_gather(both, axis, axis=dim, tiled=True), ends, axis=along))


def over_axes(x, axes):
    for axis in axes:
        x = lax.psum(x, axis)
    return x


def square_bf(values):
    wide = values.astype(jnp.float32)
    return (wide * wide).astype(jnp.bfloat16)


def accumulate(act_block, sq_block, adj_piece):
    contract = (((0,), (0,)), ((), ()))
    grad_sum = lax.dot_general(act_block, adj_piece, contract, preferred_element_type=jnp.float32)
    square_sum = lax.dot_general(
        sq_block, square_bf(adj_piece), contract, preferred_element_type=jnp.float32
    )
    return (grad_sum, square_sum)


def finish(partial_value, total_rows):
    gradient = partial_value[0] / total_rows
    precond = (partial_value[1] / total_rows + DAMPING) ** EXPONENT
    norm_term = jnp.sum(gradient * gradient / precond)
    return (gradient, precond, norm_term)


def shards(layer_input, pre_act, hidden_adjoint, output_adjoint):
    preact = pre_act.astype(jnp.float32)
    logistic = jax.nn.sigmoid(preact)
    hidden = (preact * logistic).astype(jnp.bfloat16)
    adjoint = (
        hidden_adjoint.astype(jnp.float32) * logistic * (1.0 + preact * (1.0 - logistic))
    ).astype(jnp.bfloat16)
    own_input = lax.all_to_all(layer_input, DP, split_axis=1, concat_axis=0, tiled=True)
    sq_input = square_bf(own_input)
    total_rows = own_input.shape[0]
    wide_hidden = gather_directly(hidden, "mp", 1)
    own_hidden = two_step_exchange(wide_hidden, (("dp_0", "dp_1", "dp_2"), "dp_3"), (1, 0), 1, 0)
    sq_hidden = square_bf(own_hidden)
    pieces = side_by_side((adjoint, output_adjoint), DP, 0, 1)
    first_part = accumulate(own_input, sq_input, pieces[0])
    second_part = accumulate(own_hidden, sq_hidden, pieces[1])
    gradient_in, precond_in, term_in = finish(first_part, total_rows)
    gradient_out, precond_out, term_out = finish(second_part, total_rows)
    sq_norm = over_axes(term_in + term_out, DP_MP)
    rescale = jnp.sqrt(2.0 * D * H / sq_norm)
    direction_in = gradient_in / precond_in * rescale
    direction_out = gradient_out / precond_out * rescale
    return (precond_in, direction_in, precond_out, direction_out, sq_norm)


def solution(mesh):
    torus = Mesh(
        mesh.devices.reshape(4, 4, 4, 2, mesh.shape["mp"]), ("dp_0", "dp_1", "dp_2", "dp_3", "mp")
    )
    placed = (P(DP, None), P(DP, "mp"), P(DP, "mp"), P(DP, "mp"))
    return jax.shard_map(
        shards,
        mesh=torus,
        in_specs=placed,
        out_specs=(P(DP, "mp"), P(DP, "mp"), P(DP, "mp"), P(DP, "mp"), P()),
        check_vma=False,
    )
```

profile of v0, /device:TPU:1, one launch (start us, length us, event | category | flops | bytes accessed | tf_op | source)
XLA Modules:
  0.0 209.6 jit_solution(18236963314669672673)
XLA Ops:
  7.2 0.0 all-gather.3.cloned.1.call-start
  7.2 0.8 fusion.13
  8.0 1.3 maximum_bitcast_fusion
  9.3 0.0 all-gather.3.cloned.1.call-update
  9.4 0.6 broadcast_in_dim.2
  10.0 6.4 %all-to-all-start.1 = ((bf16[4,4,2048]{2,1,0:T(4,128)(2,1)}), bf16[4,4,2048]{2,1,0:T(4,128)(2,1)S(1)}, u32[]{:S(2)}, u32[]{:S(2)}) async-start(bf16[4,4,2048]{2,1,0:T(4,128)(2,1)} %broadcast_in_dim.2), calls=%async_computation.1 | async-start | bytes 131072 | tf_op jit(solution)/shard_map/all_to_all | solution.py:25
  16.4 1.0 all_to_all.23
  17.5 0.1 copy.22
  17.6 0.7 reshape.20
  18.3 2.7 %all-to-all-done.1 = bf16[4,4,2048]{2,1,0:T(4,128)(2,1)S(1)} async-done(((bf16[4,4,2048]{2,1,0:T(4,128)(2,1)}), bf16[4,4,2048]{2,1,0:T(4,128)(2,1)S(1)}, u32[]{:S(2)}, u32[]{:S(2)}) %all-to-all-start.1) | async-done | bytes 65568 | tf_op jit(solution)/shard_map/all_to_all | solution.py:25
  21.0 0.1 copy.16
  21.1 0.2 reshape_reshape.6
  21.3 0.1 copy.21
  21.4 0.2 reshape.22
  21.5 8.3 %all_to_all.34 = bf16[2,2,8192]{2,1,0:T(2,128)(2,1)S(1)} all-to-all(bf16[2,2,8192]{2,1,0:T(2,128)(2,1)S(1)} %reshape.22), channel_id=1, replica_groups=mesh['dp_0'=4,'dp_1'=4,'dp_2'=4,'dp_3'=2,'mp'=4] {'dp_3'}, dimensions={0} | all-to-all | bytes 131072 | tf_op jit(solution)/shard_map/all_to_all | solution.py:41
  29.8 16.5 %all-to-all-start = ((bf16[128,2,128]{2,1,0:T(2,128)(2,1)}), bf16[128,2,128]{2,1,0:T(2,128)(2,1)S(1)}, u32[]{:S(2)}, u32[]{:S(2)}) async-start(bf16[128,2,128]{2,1,0:T(2,128)(2,1)} %reshape.20), calls=%async_computation | async-start | bytes 131072 | tf_op jit(solution)/shard_map/all_to_all | solution.py:94
  46.3 0.1 reshape.23
  46.5 0.8 reshape.24
  47.3 15.6 %all-to-all-done = bf16[128,2,128]{2,1,0:T(2,128)(2,1)S(1)} async-done(((bf16[128,2,128]{2,1,0:T(2,128)(2,1)}), bf16[128,2,128]{2,1,0:T(2,128)(2,1)S(1)}, u32[]{:S(2)}, u32[]{:S(2)}) %all-to-all-start) | async-done | bytes 65568 | tf_op jit(solution)/shard_map/all_to_all | solution.py:94
  63.0 5.7 %all-to-all-start.3 = ((bf16[64,2,256]{2,1,0:T(2,128)(2,1)}), bf16[64,2,256]{2,1,0:T(2,128)(2,1)S(1)}, u32[]{:S(2)}, u32[]{:S(2)}) async-start(bf16[64,2,256]{2,1,0:T(2,128)(2,1)} %reshape.24), calls=%async_computation.3 | async-start | bytes 131072 | tf_op jit(solution)/shard_map/all_to_all | solution.py:41
  68.6 0.1 reshape.21
  68.7 19.1 %all-to-all-done.3 = bf16[64,2,256]{2,1,0:T(2,128)(2,1)S(1)} async-done(((bf16[64,2,256]{2,1,0:T(2,128)(2,1)}), bf16[64,2,256]{2,1,0:T(2,128)(2,1)S(1)}, u32[]{:S(2)}, u32[]{:S(2)}) %all-to-all-start.3) | async-done | bytes 65568 | tf_op jit(solution)/shard_map/all_to_all | solution.py:41
  87.8 0.1 reshape.25
  88.0 50.1 %all-gather.3.cloned.1.call-done = bf16[128,4,4096]{2,1,0:T(4,128)(2,1)} async-done(((bf16[1,4,4096]{2,1,0:T(4,128)(2,1)}), bf16[128,4,4096]{2,1,0:T(4,128)(2,1)}) %all-gather.3.cloned.1.call-update) | async-done | bytes 4194320 | tf_op jit(solution)/shard_map/all_gather | solution.py:57
  138.1 6.9 %reshape.19 = bf16[512,4096]{1,0:T(8,128)(2,1)} reshape(bf16[128,4,4096]{2,1,0:T(4,128)(2,1)} %all-gather.3.cloned.1.call-done) | data formatting | bytes 8388608
  145.0 0.0 copy-start
  145.0 2.3 %fusion = f32[64,2048]{1,0:T(8,128)S(1)} fusion(bf16[512,4096]{1,0:T(8,128)(2,1)} %reshape.19, bf16[512,64]{1,0:T(8,128)(2,1)S(1)} %bitcast.29), kind=kOutput, calls=%fused_computation.6 | convolution fusion | flops 137723904 | bytes 2686976 | tf_op jit(solution)/shard_map/dot_general | solution.py:74
  147.3 2.9 %multiply_reduce_fusion.1 = (f32[]{:T(128)}, f32[64,2048]{1,0:T(8,128)S(1)}) fusion(f32[64,2048]{1,0:T(8,128)S(1)} %fusion, bf16[512,64]{1,0:T(8,128)(2,1)S(1)} %bitcast.30, bf16[512,4096]{1,0:T(8,128)(2,1)} %reshape.19), kind=kOutput, calls=%fused_computation.15 | convolution fusion | flops 134742016 | bytes 3211268 | tf_op jit(solution)/shard_map/dot_general | solution.py:73
  150.2 0.0 copy-done
  150.2 0.6 fusion.2
  150.8 1.2 multiply_reduce_fusion
  153.3 8.8 %psum.35 = f32[]{:T(128)} all-reduce(f32[]{:T(128)S(6)} %add.29), channel_id=1, replica_groups=mesh['dp_0'=4,'dp_1'=4,'dp_2'=4,'dp_3'=2,'mp'=4] {'dp_0'}, use_global_device_ids=true, to_apply=%region_2.0 | all-reduce | flops 1 | bytes 8 | tf_op jit(solution)/shard_map/psum | solution.py:62
  162.1 8.6 %psum.36 = f32[]{:T(128)} all-reduce(f32[]{:T(128)} %psum.35), channel_id=1, replica_groups=mesh['dp_0'=4,'dp_1'=4,'dp_2'=4,'dp_3'=2,'mp'=4] {'dp_1'}, use_global_device_ids=true, to_apply=%region_3.0 | all-reduce | flops 1 | bytes 8 | tf_op jit(solution)/shard_map/psum | solution.py:62
  170.7 13.1 %psum.37 = f32[]{:T(128)} all-reduce(f32[]{:T(128)} %psum.36), channel_id=1, replica_groups=mesh['dp_0'=4,'dp_1'=4,'dp_2'=4,'dp_3'=2,'mp'=4] {'dp_2'}, use_global_device_ids=true, to_apply=%region_4.0 | all-reduce | flops 1 | bytes 8 | tf_op jit(solution)/shard_map/psum | solution.py:62
  183.8 8.9 %psum.38 = f32[]{:T(128)} all-reduce(f32[]{:T(128)} %psum.37), channel_id=1, replica_groups=mesh['dp_0'=4,'dp_1'=4,'dp_2'=4,'dp_3'=2,'mp'=4] {'dp_3'}, use_global_device_ids=true, to_apply=%region_5.0 | all-reduce | flops 1 | bytes 8 | tf_op jit(solution)/shard_map/psum | solution.py:62
  192.7 7.3 %psum.39 = f32[]{:T(128)} all-reduce(f32[]{:T(128)} %psum.38), channel_id=1, replica_groups=mesh['dp_0'=4,'dp_1'=4,'dp_2'=4,'dp_3'=2,'mp'=4] {'mp'}, use_global_device_ids=true, to_apply=%region_6.0 | all-reduce | flops 1 | bytes 8 | tf_op jit(solution)/shard_map/psum | solution.py:62
  200.7 2.0 multiply_multiply_fusion
  (1 shorter events, 0.0 us)
Async XLA Ops:
  7.2 130.9 %all-gather.3.cloned.1.call-start = ((), (), s32[]{:S(2)}) async-start(), calls=%async_computation.4 | async-start | bytes 4227072 | tf_op jit(solution)/shard_map/all_gather | solution.py:57
  10.0 11.0 %all-to-all-start.1 = ((bf16[4,4,2048]{2,1,0:T(4,128)(2,1)}), bf16[4,4,2048]{2,1,0:T(4,128)(2,1)S(1)}, u32[]{:S(2)}, u32[]{:S(2)}) async-start(bf16[4,4,2048]{2,1,0:T(4,128)(2,1)} %broadcast_in_dim.2), calls=%async_computation.1 | async-start | bytes 131072 | tf_op jit(solution)/shard_map/all_to_all | solution.py:25
  29.8 33.2 %all-to-all-start = ((bf16[128,2,128]{2,1,0:T(2,128)(2,1)}), bf16[128,2,128]{2,1,0:T(2,128)(2,1)S(1)}, u32[]{:S(2)}, u32[]{:S(2)}) async-start(bf16[128,2,128]{2,1,0:T(2,128)(2,1)} %reshape.20), calls=%async_computation | async-start | bytes 131072 | tf_op jit(solution)/shard_map/all_to_all | solution.py:94
  63.0 24.9 %all-to-all-start.3 = ((bf16[64,2,256]{2,1,0:T(2,128)(2,1)}), bf16[64,2,256]{2,1,0:T(2,128)(2,1)S(1)}, u32[]{:S(2)}, u32[]{:S(2)}) async-start(bf16[64,2,256]{2,1,0:T(2,128)(2,1)} %reshape.24), calls=%async_computation.3 | async-start | bytes 131072 | tf_op jit(solution)/shard_map/all_to_all | solution.py:41
  145.0 5.2 %copy-start = (bf16[512,4096]{1,0:T(8,128)(2,1)S(1)}, bf16[512,4096]{1,0:T(8,128)(2,1)}, u32[]{:S(2)}) copy-start(bf16[512,4096]{1,0:T(8,128)(2,1)} %reshape.19) | copy-start | bytes 12582916
Sparse Core Ops, SparseCore 0:
  13.0 125.0 all-gather.2
where the time goes:
time: 211 us; the launch traced here: 210 us
  waiting for transfers between devices  87.6 us (42%)
  blocking collectives  54.9 us (26%)
  starting transfers between devices  28.7 us (14%)
  between operations  16.1 us (8%)
  local copies, waits for them, and re-layouts  11.1 us (5%)
  matrix products  7.01 us (3%)
  other arithmetic  4.16 us (2%)
    all_gather x1, waiting for transfers between devices, side_by_side(): lax.all_gather(both, axis, axis=dim, tiled=True)  50.1 us
    psum x5, blocking collectives, over_axes(): x = lax.psum(x, axis)  46.6 us
    all_to_all x1, waiting for transfers between devices, exchange_in_order(): lax.all_to_all(pieces, axes[k], split_axis=k, concat_axis=k, tiled=True)  19.1 us
    all_to_all x1, starting transfers between devices, shards(): lax.all_to_all(layer_input, DP, split_axis=1, concat_axis=0, tiled=True)  16.5 us
    all_to_all x1, waiting for transfers between devices, shards(): lax.all_to_all(layer_input, DP, split_axis=1, concat_axis=0, tiled=True)  15.6 us
    unnamed x9, local copies, waits for them, and re-layouts  8.99 us
    all_to_all x1, blocking collectives, exchange_in_order(): lax.all_to_all(pieces, axes[k], split_axis=k, concat_axis=k, tiled=True)  8.26 us
    all_to_all x1, starting transfers between devices, copy_for_each(): lax.all_to_all(jnp.broadcast_to(x[None], (size, *x.shape)), axis, 0, 0, t...  6.43 us
  transfers between devices with their start and end apart: 4, of which 4 were waited for; matrix products, arithmetic and copies ran while one was open for 2% of the time, Pallas kernels for 0%

commit v1 on v0

v1 whole, which is shorter than its diff:
```python
import jax
import jax.numpy as jnp
from jax import lax
from jax.experimental import pallas as pl
from jax.experimental.pallas import tpu as pltpu
from jax.sharding import Mesh
from jax.sharding import PartitionSpec as P

D = 8192
H = 8192
EXAMPLES = 512
DP = ("dp_0", "dp_1", "dp_2", "dp_3")
AXES = ("dp_0", "dp_1", "dp_2", "dp_3", "mp")
MESH = pl.DeviceIdType.MESH
BF = jnp.bfloat16
F32 = jnp.float32

DAMPING = 0.1
EXPONENT = 0.75

N_PAIR = 1
N_MSG = 128
TILE = 256


def mod4(a):
    return lax.rem(a, 4)


def sq_round(v):
    w = v.astype(F32)
    return (w * w).astype(BF)


def kernel(
    li_hbm, pre_hbm, ha_hbm, oa_hbm,
    p_out, r_out, n_out,
    pre_v, ha_v, oa_v, hid, stack, pair_src, pair_dst, pair_f32,
    big, v1, v2, v3, tile_f32, lhs, lhs_t, lhs_sq, acc_g, acc_s, norm_acc, red_a, red_b,
    in_sem, send_sem, recv_sem, li_send, li_recv, hid_send, hid_recv, red_send, red_recv,
):
    y, x, zh, c, zl = (lax.axis_index(a) for a in AXES)
    d = 1 - c
    f = x * d + y * c
    s = y * d + x * c
    fp, fm, fo = mod4(f + 1), mod4(f + 3), mod4(f + 2)
    sp, sm, so = mod4(s + 1), mod4(s + 3), mod4(s + 2)
    zp, zm, zo = mod4(zh + 1), mod4(zh + 3), mod4(zh + 2)

    def at_f(fd):
        return (y * d + fd * c, fd * d + x * c, zh, c, zl)

    def at_s(sd):
        return (sd * d + y * c, x * d + sd * c, zh, c, zl)

    def at_z(zd):
        return (y, x, zd, c, zl)

    partner = (y, x, zh, d, zl)

    loads = [
        pltpu.make_async_copy(pre_hbm, pre_v, in_sem.at[0]),
        pltpu.make_async_copy(ha_hbm, ha_v, in_sem.at[1]),
        pltpu.make_async_copy(oa_hbm, oa_v, in_sem.at[2]),
    ]
    for load in loads:
        load.start()

    barrier = pltpu.get_barrier_semaphore()

    def hello(device):
        pl.semaphore_signal(barrier, inc=1, device_id=device, device_id_type=MESH)

    hello(partner)
    for k in (1, 2, 3):
        hello((mod4(y + k), x, zh, c, zl))
        hello((y, mod4(x + k), zh, c, zl))
    hello(at_z(zp))
    hello(at_z(zm))
    for ys in range(4):
        own = jnp.logical_and(y == ys, zl == y)

        @pl.when(jnp.logical_not(own))
        def _():
            hello((ys, x, zh, c, y))

    for load in loads:
        load.wait()
    preact = pre_v[...].astype(F32)
    logistic = 1.0 / (1.0 + jnp.exp(-preact))
    hid[...] = (preact * logistic).astype(BF)
    adjoint = (ha_v[...].astype(F32) * logistic * (1.0 + preact * (1.0 - logistic))).astype(BF)
    stack[0:4, :] = adjoint.astype(F32)
    stack[4:8, :] = oa_v[...].astype(F32)
    pair_src[0] = stack[:, 0:1024].astype(BF)
    pair_src[1] = stack[:, 1024:2048].astype(BF)

    pl.semaphore_wait(barrier, 13 - jnp.where(y == zl, 1, 0).astype(jnp.int32))

    sent = []

    def send(src, dst, device):
        i = len(sent)
        copy = pltpu.make_async_remote_copy(
            src_ref=src, dst_ref=dst, send_sem=send_sem.at[i], recv_sem=recv_sem.at[i],
            device_id=device, device_id_type=MESH,
        )
        copy.start()
        sent.append(copy)
        return copy

    exchange = send(pair_src.at[d], pair_dst, partner)

    li_copies = []
    for k in (1, 2, 3):
        yd = mod4(y + k)
        cols = pl.ds(pl.multiple_of(yd * 2048, 2048), 2048)
        copy = pltpu.make_async_remote_copy(
            src_ref=li_hbm.at[:, cols], dst_ref=v1.at[y], send_sem=li_send.at[k - 1],
            recv_sem=li_recv.at[k - 1], device_id=(yd, x, zh, c, zl), device_id_type=MESH,
        )
        copy.start()
        li_copies.append(copy)
    li_own = pltpu.make_async_copy(
        li_hbm.at[:, pl.ds(pl.multiple_of(y * 2048, 2048), 2048)], v1.at[y], in_sem.at[0]
    )
    li_own.start()
    hid_copies = []
    for zd in range(4):
        own = jnp.logical_and(y == zl, zl == zd)
        remote = pltpu.make_async_remote_copy(
            src_ref=hid, dst_ref=v1.at[4 + y], send_sem=hid_send.at[zd],
            recv_sem=hid_recv.at[y], device_id=(zl, x, zh, c, zd), device_id_type=MESH,
        )
        local = pltpu.make_async_copy(hid, v1.at[4 + y], hid_recv.at[y])
        hid_copies.append((own, remote))

        @pl.when(own)
        def _():
            local.start()

        @pl.when(jnp.logical_not(own))
        def _():
            remote.start()

    exchange.wait_recv()
    mine = pair_src[c].astype(F32)
    other = pair_dst[...].astype(F32)
    first = c == 0
    pair_f32[0:8, :] = jnp.where(first, mine, other)
    pair_f32[8:16, :] = jnp.where(first, other, mine)
    big[c, zh, s, f] = pair_f32[...].astype(BF)

    def block(z, sd, fd):
        return big.at[c, z, sd, fd]

    def half(z, sd, fd, k):
        return big.at[c, z, sd, fd, :, pl.ds(512 * k, 512)]

    z1p = send(block(zh, s, f), block(zh, s, f), at_z(zp))
    z1m = send(block(zh, s, f), block(zh, s, f), at_z(zm))

    slices = (zh, zm, zp, zo)
    F1, F2, S1, S2, X = {}, {}, {}, {}, {}

    def both_s(k, j, fd):
        z = slices[k]
        S1[k, j, 0] = send(block(z, s, fd), block(z, s, fd), at_s(sp))
        S1[k, j, 1] = send(block(z, s, fd), block(z, s, fd), at_s(sm))

    def stage_a(k):
        z = slices[k]
        F1[k, 0] = send(block(z, s, f), block(z, s, f), at_f(fp))
        F1[k, 1] = send(block(z, s, f), block(z, s, f), at_f(fm))
        both_s(k, 0, f)

    def stage_b(k):
        z = slices[k]
        F1[k, 0].wait_recv()
        F2[k, 0] = send(half(z, s, fm, 0), half(z, s, fm, 0), at_f(fp))
        F1[k, 1].wait_recv()
        F2[k, 1] = send(half(z, s, fp, 1), half(z, s, fp, 1), at_f(fm))
        both_s(k, 1, fm)
        both_s(k, 2, fp)

    def stage_c(k):
        z = slices[k]
        S1[k, 0, 0].wait_recv()
        S2[k, 0] = send(block(z, sm, f), block(z, sm, f), at_s(sp))

    def stage_d(k):
        F2[k, 0].wait_recv()
        F2[k, 1].wait_recv()
        both_s(k, 3, fo)

    def stage_e(k):
        z = slices[k]
        S1[k, 1, 0].wait_recv()
        S2[k, 1] = send(block(z, sm, fm), block(z, sm, fm), at_s(sp))
        S1[k, 2, 1].wait_recv()
        S2[k, 2] = send(block(z, sp, fp), block(z, sp, fp), at_s(sm))

    def stage_f(k):
        z = slices[k]
        S1[k, 3, 1].wait_recv()
        S2[k, 3] = send(block(z, sp, fo), block(z, sp, fo), at_s(sm))

    def stage_g(k):
        z = slices[k]
        S1[k, 0, 1].wait_recv()
        S1[k, 1, 1].wait_recv()
        S1[k, 2, 0].wait_recv()
        S1[k, 3, 0].wait_recv()
        for j in range(4):
            S2[k, j].wait_recv()
        X[k] = send(big.at[c, z], big.at[c, z], partner)

    def rows_x():
        for copy in li_copies:
            copy.wait_recv()
        li_own.wait()
        for ys in range(4):
            pltpu.make_async_copy(hid, v1.at[4 + ys], hid_recv.at[ys]).wait()
        copies = []
        for k in (1, 2, 3):
            xd = mod4(x + k)
            cols = pl.ds(pl.multiple_of(xd * 512, 512), 512)
            copies.append(send(v1.at[:, :, cols], v2.at[x], (y, xd, zh, c, zl)))
        local = pltpu.make_async_copy(
            v1.at[:, :, pl.ds(pl.multiple_of(x * 512, 512), 512)], v2.at[x], in_sem.at[1]
        )
        local.start()
        return copies, local

    def rows_z(copies, local):
        for copy in copies:
            copy.wait_recv()
        local.wait()
        out = []
        for k in (1, 2, 3):
            zd = mod4(zh + k)
            cols = pl.ds(pl.multiple_of(zd * 128, 128), 128)
            out.append(send(v2.at[:, :, :, cols], v3.at[c, zh], at_z(zd)))
        local = pltpu.make_async_copy(
            v2.at[:, :, :, pl.ds(pl.multiple_of(zh * 128, 128), 128)], v3.at[c, zh], in_sem.at[2]
        )
        local.start()
        return out, local

    def rows_core(copies, local):
        for copy in copies:
            copy.wait_recv()
        local.wait()
        return send(v3.at[c], v3.at[c], partner)

    stage_a(0)
    stage_b(0)
    stage_c(0)
    z1p.wait_recv()
    z2p = send(half(zm, s, f, 0), half(zm, s, f, 0), at_z(zp))
    z1m.wait_recv()
    z2m = send(half(zp, s, f, 1), half(zp, s, f, 1), at_z(zm))
    stage_a(1)
    stage_a(2)
    stage_d(0)
    stage_e(0)
    rows = rows_x()
    stage_b(1)
    stage_b(2)
    stage_c(1)
    stage_c(2)
    stage_f(0)
    stage_d(1)
    stage_d(2)
    z2p.wait_recv()
    z2m.wait_recv()
    stage_a(3)
    rows = rows_z(*rows)
    stage_e(1)
    stage_e(2)
    stage_g(0)
    stage_b(3)
    stage_c(3)
    stage_f(1)
    stage_f(2)
    stage_d(3)
    stage_g(1)
    stage_g(2)
    stage_e(3)
    last_rows = rows_core(*rows)
    stage_f(3)

    last_rows.wait_recv()
    row = lax.broadcasted_iota(jnp.int32, (16, 128), 0)
    lane = lax.broadcasted_iota(jnp.int32, (16, 128), 1)
    kind = lax.rem(row // 4, 2)
    side = lane // 64
    keep = kind == side
    straight = side == c

    @pl.loop(0, 64)
    def _(i):
        z, xs, ys = i // 16, lax.rem(i // 4, 4), lax.rem(i, 4)
        for q in range(4):
            core, kd = divmod(q, 2)
            tile_f32[4 * q : 4 * q + 4, :] = v3[core, z, xs, kd * 4 + ys].astype(F32)
        data = tile_f32[...]
        turned = pltpu.roll(data, 64, 1)
        rows16 = jnp.where(keep, jnp.where(straight, data, turned), 0.0).astype(BF)
        lhs[0, z, ys * 4 + xs] = rows16
        lhs[1, z, xs * 4 + ys] = rows16

    for cc in range(2):
        for z in range(4):
            t = jnp.transpose(lhs[cc, z].reshape(256, 128).astype(F32))
            lhs_t[cc, z] = t.astype(BF)
            lhs_sq[cc, z] = (t * t).astype(BF)

    def dots(cc, z, cols):
        right = big[cc, z, :, :, :, cols].reshape(256, TILE)
        grad = jnp.dot(lhs_t[cc, z], right, preferred_element_type=F32)
        square = jnp.dot(lhs_sq[cc, z], sq_round(right), preferred_element_type=F32)
        return grad, square

    for k in range(3):
        X[k].wait_recv()

    for cc in range(2):

        @pl.loop(0, 1024 // TILE)
        def _(j):
            cols = pl.ds(pl.multiple_of(j * TILE, TILE), TILE)
            wide = pl.ds(pl.multiple_of(cc * 1024 + j * TILE, TILE), TILE)
            parts = [dots(cc, slices[k], cols) for k in range(3)]
            acc_g[:, wide] = parts[0][0] + parts[1][0] + parts[2][0]
            acc_s[:, wide] = parts[0][1] + parts[1][1] + parts[2][1]

    stage_g(3)
    X[3].wait_recv()
    norm_acc[...] = jnp.zeros_like(norm_acc)
    for cc in range(2):

        @pl.loop(0, 1024 // TILE)
        def _(j):
            cols = pl.ds(pl.multiple_of(j * TILE, TILE), TILE)
            wide = pl.ds(pl.multiple_of(cc * 1024 + j * TILE, TILE), TILE)
            grad, square = dots(cc, zo, cols)
            grad = (acc_g[:, wide] + grad) / EXAMPLES
            base = (acc_s[:, wide] + square) / EXAMPLES + DAMPING
            precond = jnp.exp(EXPONENT * jnp.log(base))
            ratio = grad / precond
            p_out[:, wide] = precond
            r_out[:, wide] = ratio
            norm_acc[...] += jnp.sum(grad * ratio, axis=0, keepdims=True)

    own_norm = jnp.sum(norm_acc[...], axis=1, keepdims=True)
    plane = (y * 4 + x) * 2 + c
    red_a[plane] = jnp.broadcast_to(own_norm, (1, 128))

    @pl.loop(1, 32)
    def _(k):
        to = lax.rem(plane + k, 32)
        pltpu.make_async_remote_copy(
            src_ref=red_a.at[plane], dst_ref=red_a.at[plane], send_sem=red_send.at[0],
            recv_sem=red_recv.at[0],
            device_id=(to // 8, lax.rem(to // 2, 4), zh, lax.rem(to, 2), zl), device_id_type=MESH,
        ).start()

    pltpu.make_async_copy(red_a.at[pl.ds(0, 31)], red_a.at[pl.ds(0, 31)], red_recv.at[0]).wait()
    z16 = zh * 4 + zl
    red_b[z16] = jnp.sum(red_a[...], axis=0)

    @pl.loop(1, 16)
    def _(k):
        to = lax.rem(z16 + k, 16)
        pltpu.make_async_remote_copy(
            src_ref=red_b.at[z16], dst_ref=red_b.at[z16], send_sem=red_send.at[1],
            recv_sem=red_recv.at[1],
            device_id=(y, x, to // 4, c, lax.rem(to, 4)), device_id_type=MESH,
        ).start()

    for copy in sent:
        copy.wait_send()
    for copy in li_copies:
        copy.wait_send()
    for own, remote in hid_copies:

        @pl.when(jnp.logical_not(own))
        def _():
            remote.wait_send()

    pltpu.make_async_copy(red_a.at[pl.ds(0, 31)], red_a.at[pl.ds(0, 31)], red_send.at[0]).wait()
    pltpu.make_async_copy(red_b.at[pl.ds(0, 15)], red_b.at[pl.ds(0, 15)], red_recv.at[1]).wait()
    n_out[...] = jnp.sum(red_b[...], axis=0)
    pltpu.make_async_copy(red_b.at[pl.ds(0, 15)], red_b.at[pl.ds(0, 15)], red_send.at[1]).wait()


def shards(layer_input, pre_act, hidden_adjoint, output_adjoint):
    any_space = pl.BlockSpec(memory_space=pl.ANY)
    vmem = pl.BlockSpec(memory_space=pltpu.VMEM)
    dma = pltpu.SemaphoreType.DMA
    precond, ratio, norm = pl.pallas_call(
        kernel,
        out_shape=(
            jax.ShapeDtypeStruct((128, 2048), F32),
            jax.ShapeDtypeStruct((128, 2048), F32),
            jax.ShapeDtypeStruct((1, 128), F32),
        ),
        in_specs=[any_space] * 4,
        out_specs=(vmem, vmem, vmem),
        scratch_shapes=[
            pltpu.VMEM((4, 2048), BF),
            pltpu.VMEM((4, 2048), BF),
            pltpu.VMEM((4, 2048), BF),
            pltpu.VMEM((4, 2048), BF),
            pltpu.VMEM((8, 2048), F32),
            pltpu.VMEM((2, 8, 1024), BF),
            pltpu.VMEM((8, 1024), BF),
            pltpu.VMEM((16, 1024), F32),
            pltpu.VMEM((2, 4, 4, 4, 16, 1024), BF),
            pltpu.VMEM((8, 4, 2048), BF),
            pltpu.VMEM((4, 8, 4, 512), BF),
            pltpu.VMEM((2, 4, 4, 8, 4, 128), BF),
            pltpu.VMEM((16, 128), F32),
            pltpu.VMEM((2, 4, 16, 16, 128), BF),
            pltpu.VMEM((2, 4, 128, 256), BF),
            pltpu.VMEM((2, 4, 128, 256), BF),
            pltpu.VMEM((128, 2048), F32),
            pltpu.VMEM((128, 2048), F32),
            pltpu.VMEM((1, TILE), F32),
            pltpu.VMEM((32, 1, 128), F32),
            pltpu.VMEM((16, 1, 128), F32),
            dma((3,)),
            dma((N_MSG,)),
            dma((N_MSG,)),
            dma((3,)),
            dma((3,)),
            dma((4,)),
            dma((4,)),
            dma((2,)),
            dma((2,)),
        ],
        compiler_params=pltpu.CompilerParams(collective_id=0, has_side_effects=True),
    )(layer_input, pre_act, hidden_adjoint, output_adjoint)
    sq_norm = norm[0, 0]
    rescale = jnp.sqrt(2.0 * D * H / sq_norm)
    return (
        precond[:64],
        ratio[:64] * rescale,
        precond[64:],
        ratio[64:] * rescale,
        sq_norm,
    )


def solution(mesh):
    torus = Mesh(mesh.devices.reshape(4, 4, 4, 2, mesh.shape["mp"]), AXES)
    placed = (P(DP, None), P(DP, "mp"), P(DP, "mp"), P(DP, "mp"))
    return jax.shard_map(
        shards,
        mesh=torus,
        in_specs=placed,
        out_specs=(P(DP, "mp"), P(DP, "mp"), P(DP, "mp"), P(DP, "mp"), P()),
        check_vma=False,
    )
```

time: 211 us -> 73.3 us (0.35)
  waiting for transfers between devices: 87.6 us -> 0 us
  Pallas kernels: 0 us -> 67.6 us
  blocking collectives: 54.9 us -> 0 us
  starting transfers between devices: 28.7 us -> 0 us
  between operations: 16.1 us -> 1.94 us
  local copies, waits for them, and re-layouts: 11.1 us -> 0.57 us
  matrix products: 7.01 us -> 0 us
    pallas_call x0 -> x1, Pallas kernels: none -> 67.6 us  [shards(): pl.pallas_call(kernel, out_shape=(jax.ShapeDtypeStruct((128, 2048), F32),...]
    all_gather x1 -> x0, waiting for transfers between devices: 50.1 us -> none  [side_by_side(): lax.all_gather(both, axis, axis=dim, tiled=True)]
    psum x5 -> x0, blocking collectives: 46.6 us -> none  [over_axes(): x = lax.psum(x, axis)]
    all_to_all x3 -> x0, waiting for transfers between devices: 37.5 us -> none  [the longest x1 19.1 us: exchange_in_order(): lax.all_to_all(pieces, axes[k], split_axis=k, concat_axis=k, tiled=True)]
    all_to_all x3 -> x0, starting transfers between devices: 28.6 us -> none  [the longest x1 16.5 us: shards(): lax.all_to_all(layer_input, DP, split_axis=1, concat_axis=0, tiled=True)]
    unnamed x9 -> x2, local copies, waits for them, and re-layouts: 8.99 us -> 0.57 us
    all_to_all x1 -> x0, blocking collectives: 8.26 us -> none  [exchange_in_order(): lax.all_to_all(pieces, axes[k], split_axis=k, concat_axis=k, tiled=True)]
    dot_general x4 -> x0, matrix products: 7.01 us -> none  [the longest x2 4.11 us: accumulate(): lax.dot_general(act_block, adj_piece, contract, preferred_element_type=jn...]
  transfers between devices with their start and end apart: 4 -> 0, of which waited for: 4 -> 0; matrix products, arithmetic and copies ran while one was open for 2% -> 0% of each run, Pallas kernels for 0% -> 0%
where the time goes in v1:
time: 73.3 us; the launch traced here: 73 us
  Pallas kernels  67.6 us (92%)
  other arithmetic  2.88 us (4%)
  between operations  1.94 us (3%)
    pallas_call x1, Pallas kernels, shards(): pl.pallas_call(kernel, out_shape=(jax.ShapeDtypeStruct((128, 2048), F32),...  67.6 us
    mul x1, other arithmetic, shards(): ratio[64:] * rescale  2.88 us

profile of v1, /device:TPU:1, one launch (start us, length us, event | category | flops | bytes accessed | tf_op | source)
XLA Modules:
  0.0 73.0 jit_solution(1899639512664991524)
XLA Ops:
  0.6 67.6 %shard_map.83 = (f32[128,2048]{1,0:T(8,128)}, f32[128,2048]{1,0:T(8,128)}, f32[1,128]{1,0:T(1,128)}) custom-call(bf16[4,8192]{1,0:T(4,128)(2,1)} %li_hbm.1, bf16[4,2048]{1,0:T(4,128)(2,1)} %pre_hbm.1, bf16[4,2048]{1,0:T(4,128)(2,1)} %ha_hbm.1, bf16[4,2048]{1,0:T(4,128)(2,1)} %oa_hbm.1), custom_call_target="tpu_custom_call" | custom-call | tf_op jit(solution)/shard_map/pallas_call | solution.py:402
  68.2 0.0 copy-start
  68.2 0.6 copy-done
  68.9 2.9 %slice_multiply_fusion = (f32[64,2048]{1,0:T(8,128)}, f32[64,2048]{1,0:T(8,128)}, f32[64,2048]{1,0:T(8,128)}, f32[64,2048]{1,0:T(8,128)}) fusion(f32[128,2048]{1,0:T(8,128)} %get-tuple-element.9, f32[]{:T(128)S(6)} %sqrt.3, f32[128,2048]{1,0:T(8,128)} %get-tuple-element.8), kind=kLoop, calls=%fused_computation | loop fusion | flops 262144 | bytes 4194308 | tf_op jit(solution)/shard_map/mul | solution.py:451
Async XLA Ops:
  68.2 0.6 copy-start

commit v2 on v1

v2 whole, which is shorter than its diff:
```python
import jax
import jax.numpy as jnp
from jax import lax
from jax.experimental import pallas as pl
from jax.experimental.pallas import tpu as pltpu
from jax.sharding import Mesh
from jax.sharding import PartitionSpec as P

D = 8192
H = 8192
EXAMPLES = 512
DP = ("dp_0", "dp_1", "dp_2", "dp_3")
AXES = ("dp_0", "dp_1", "dp_2", "dp_3", "mp")
MESH = pl.DeviceIdType.MESH
BF = jnp.bfloat16
F32 = jnp.float32

DAMPING = 0.1
EXPONENT = 0.75

N_MSG = 128
TILE = 256
K1_LIMIT = 32 * 1024 * 1024


def mod4(a):
    return lax.rem(a, 4)


def sq_round(v):
    w = v.astype(F32)
    return (w * w).astype(BF)


def kernel(
    li_hbm, pre_hbm, ha_hbm, oa_hbm,
    p_all, r_all, n_out,
    pre_v, ha_v, oa_v, li_v, stack, rows0, pair_src, pair_dst,
    big, rows1, rows2, rows3, lhs_t, lhs_sq, acc_g, acc_s, norm_acc, red_a, red_b,
    in_sem, send_sem, recv_sem, out_send, out_recv, red_send, red_recv, hello_sem,
):
    y, x, zh, c, zl = (lax.axis_index(a) for a in AXES)
    d = 1 - c
    f = x * d + y * c
    s = y * d + x * c
    fp, fm, fo = mod4(f + 1), mod4(f + 3), mod4(f + 2)
    sp, sm, so = mod4(s + 1), mod4(s + 3), mod4(s + 2)
    zp, zm, zo = mod4(zh + 1), mod4(zh + 3), mod4(zh + 2)

    def at_f(fd):
        return (y * d + fd * c, fd * d + x * c, zh, c, zl)

    def at_s(sd):
        return (sd * d + y * c, x * d + sd * c, zh, c, zl)

    def at_z(zd):
        return (y, x, zd, c, zl)

    partner = (y, x, zh, d, zl)

    barrier = pltpu.get_barrier_semaphore()

    def tell(semaphore, device):
        pl.semaphore_signal(semaphore, inc=1, device_id=device, device_id_type=MESH)

    tell(barrier, at_z(zp))
    tell(barrier, at_z(zm))
    for k in (1, 2, 3):
        tell(barrier, (y, x, zh, c, mod4(zl + k)))
        tell(barrier, (mod4(y + k), x, zh, c, zl))
        tell(barrier, (y, mod4(x + k), zh, c, zl))
    tell(barrier, partner)

    loads = [
        pltpu.make_async_copy(pre_hbm, pre_v, in_sem.at[0]),
        pltpu.make_async_copy(ha_hbm, ha_v, in_sem.at[1]),
        pltpu.make_async_copy(oa_hbm, oa_v, in_sem.at[2]),
        pltpu.make_async_copy(
            li_hbm.at[:, pl.ds(pl.multiple_of(zl * 2048, 2048), 2048)], li_v, in_sem.at[3]
        ),
    ]
    for load in loads:
        load.start()
    for load in loads:
        load.wait()
    preact = pre_v[...].astype(F32)
    logistic = 1.0 / (1.0 + jnp.exp(-preact))
    hidden = (preact * logistic).astype(BF)
    adjoint = (ha_v[...].astype(F32) * logistic * (1.0 + preact * (1.0 - logistic))).astype(BF)
    stack[0, 0:4, :] = adjoint.astype(F32)
    stack[0, 4:8, :] = oa_v[...].astype(F32)
    stack[1, 0:4, :] = li_v[...].astype(F32)
    stack[1, 4:8, :] = hidden.astype(F32)
    pair_src[0] = stack[0, :, 0:1024].astype(BF)
    pair_src[1] = stack[0, :, 1024:2048].astype(BF)
    for k in range(4):
        rows0[k] = stack[1, :, 512 * k : 512 * (k + 1)].astype(BF)

    pl.semaphore_wait(barrier, 12)

    sent = []

    def send(src, dst, device):
        i = len(sent)
        copy = pltpu.make_async_remote_copy(
            src_ref=src, dst_ref=dst, send_sem=send_sem.at[i], recv_sem=recv_sem.at[i],
            device_id=device, device_id_type=MESH,
        )
        copy.start()
        sent.append(copy)
        return copy

    exchange = send(pair_src.at[d], pair_dst, partner)
    row_hop = []
    for k in (1, 2, 3):
        xd = mod4(x + k)
        row_hop.append(send(rows0.at[xd], rows1.at[x], (y, xd, zh, c, zl)))
    row_own = pltpu.make_async_copy(rows0.at[x], rows1.at[x], in_sem.at[0])
    row_own.start()
    tell(hello_sem.at[0], at_z(zp))
    for k in (1, 2, 3):
        tell(hello_sem.at[1], (mod4(y + k), x, zh, c, zl))

    def rows_z(copies, local):
        for copy in copies:
            copy.wait_recv()
        local.wait()
        pl.semaphore_wait(hello_sem.at[0], 1)
        out = []
        for k in (2, 1, 3):
            zd = mod4(zh + k)
            cols = pl.ds(pl.multiple_of(zd * 128, 128), 128)
            out.append(send(rows1.at[:, :, cols], rows2.at[zh], at_z(zd)))
        local = pltpu.make_async_copy(
            rows1.at[:, :, pl.ds(pl.multiple_of(zh * 128, 128), 128)], rows2.at[zh], in_sem.at[1]
        )
        local.start()
        return out, local

    def rows_y(copies, local):
        for copy in copies:
            copy.wait_recv()
        local.wait()
        pl.semaphore_wait(hello_sem.at[1], 3)
        out = []
        for zd in range(4):
            own = jnp.logical_and(y == zl, zl == zd)
            remote = pltpu.make_async_remote_copy(
                src_ref=rows2, dst_ref=rows3.at[c, y], send_sem=out_send.at[zd],
                recv_sem=out_recv.at[y], device_id=(zl, x, zh, c, zd), device_id_type=MESH,
            )
            out.append((own, remote))

            @pl.when(own)
            def _():
                pltpu.make_async_copy(rows2, rows3.at[c, y], out_recv.at[y]).start()

            @pl.when(jnp.logical_not(own))
            def _():
                remote.start()

        return out

    def rows_core():
        for ys in range(4):
            pltpu.make_async_copy(rows2, rows3.at[c, ys], out_recv.at[ys]).wait()
        return send(rows3.at[c], rows3.at[c], partner)

    def block(z, sd, fd):
        return big.at[c, z, sd * d + fd * c, fd * d + sd * c]

    def half(z, sd, fd, k):
        return big.at[c, z, sd * d + fd * c, fd * d + sd * c, :, pl.ds(512 * k, 512)]

    slices = (zh, zm, zp, zo)
    F1, F2, S1, S2, X = {}, {}, {}, {}, {}

    def both_s(k, j, fd):
        z = slices[k]
        S1[k, j, 0] = send(block(z, s, fd), block(z, s, fd), at_s(sp))
        S1[k, j, 1] = send(block(z, s, fd), block(z, s, fd), at_s(sm))

    def stage_a(k):
        z = slices[k]
        F1[k, 0] = send(block(z, s, f), block(z, s, f), at_f(fp))
        F1[k, 1] = send(block(z, s, f), block(z, s, f), at_f(fm))
        both_s(k, 0, f)
        F2[k] = send(block(z, s, f), block(z, s, f), at_f(fo))

    def stage_b(k):
        F1[k, 0].wait_recv()
        both_s(k, 1, fm)
        F1[k, 1].wait_recv()
        both_s(k, 2, fp)

    def stage_c(k):
        z = slices[k]
        S1[k, 0, 0].wait_recv()
        S2[k, 0] = send(block(z, sm, f), block(z, sm, f), at_s(sp))

    def stage_d(k):
        F2[k].wait_recv()
        both_s(k, 3, fo)

    def stage_e(k):
        z = slices[k]
        S1[k, 1, 0].wait_recv()
        S2[k, 1] = send(block(z, sm, fm), block(z, sm, fm), at_s(sp))
        S1[k, 2, 1].wait_recv()
        S2[k, 2] = send(block(z, sp, fp), block(z, sp, fp), at_s(sm))

    def stage_f(k):
        z = slices[k]
        S1[k, 3, 1].wait_recv()
        S2[k, 3] = send(block(z, sp, fo), block(z, sp, fo), at_s(sm))

    def stage_g(k):
        z = slices[k]
        S1[k, 0, 1].wait_recv()
        S1[k, 1, 1].wait_recv()
        S1[k, 2, 0].wait_recv()
        S1[k, 3, 0].wait_recv()
        for j in range(4):
            S2[k, j].wait_recv()
        X[k] = send(big.at[c, z], big.at[c, z], partner)

    def finish_rows(last):
        last.wait_recv()
        row = lax.broadcasted_iota(jnp.int32, (256, 128), 0)
        lane = lax.broadcasted_iota(jnp.int32, (256, 128), 1)
        keep = lax.rem(row // 4, 2) == lane // 64
        straight = lane // 64 == c

        @pl.loop(0, 4)
        def _(z):
            parts = [rows3[core, :, z].reshape(16, 8, 128).astype(F32) for core in range(2)]
            data = jnp.stack(parts, axis=1).reshape(256, 128)
            turned = pltpu.roll(data, 64, 1)
            t = jnp.transpose(jnp.where(keep, jnp.where(straight, data, turned), 0.0))
            lhs_t[z] = t.astype(BF)
            lhs_sq[z] = (t * t).astype(BF)

    def dots(zs, j):
        cols = pl.ds(pl.multiple_of(lax.rem(j, 4) * TILE, TILE), TILE)
        rights = [big[j // 4, z, :, :, :, cols].reshape(256, TILE) for z in zs]
        right = jnp.concatenate(rights, axis=0)
        left = jnp.concatenate([lhs_t[z] for z in zs], axis=1)
        left_sq = jnp.concatenate([lhs_sq[z] for z in zs], axis=1)
        grad = jnp.dot(left, right, preferred_element_type=F32)
        square = jnp.dot(left_sq, sq_round(right), preferred_element_type=F32)
        return grad, square

    def mm_first(ks):
        for k in ks:
            X[k].wait_recv()

        @pl.loop(0, 8)
        def _(j):
            grad, square = dots([slices[k] for k in ks], j)
            wide = pl.ds(pl.multiple_of(j * TILE, TILE), TILE)
            acc_g[:, wide] = grad
            acc_s[:, wide] = square

    def mm_last():
        X[3].wait_recv()
        norm_acc[...] = jnp.zeros_like(norm_acc)

        @pl.loop(0, 8)
        def _(j):
            grad, square = dots([zo], j)
            wide = pl.ds(pl.multiple_of(j * TILE, TILE), TILE)
            grad = (acc_g[:, wide] + grad) / EXAMPLES
            base = (acc_s[:, wide] + square) / EXAMPLES + DAMPING
            precond = jnp.exp(EXPONENT * jnp.log(base))
            ratio = grad / precond
            p_all[:, wide] = precond
            r_all[:, wide] = ratio
            norm_acc[...] += jnp.sum(grad * ratio, axis=0, keepdims=True)

    exchange.wait_recv()
    first = c == 0
    mine = pair_src[c].astype(F32)
    other = pair_dst[...].astype(F32)
    low, high = jnp.where(first, mine, other), jnp.where(first, other, mine)
    big[c, zh, y, x] = jnp.concatenate([low, high], axis=0).astype(BF)

    z1a = send(half(zh, s, f, 0), half(zh, s, f, 0), at_z(zp))
    z1b = send(half(zh, s, f, 1), half(zh, s, f, 1), at_z(zm))
    stage_a(0)
    z1c = send(half(zh, s, f, 1), half(zh, s, f, 1), at_z(zp))
    z1d = send(half(zh, s, f, 0), half(zh, s, f, 0), at_z(zm))
    row_copies = rows_z(row_hop, row_own)
    stage_b(0)
    stage_c(0)
    z1a.wait_recv()
    z2p = send(half(zm, s, f, 0), half(zm, s, f, 0), at_z(zp))
    z1b.wait_recv()
    z2m = send(half(zp, s, f, 1), half(zp, s, f, 1), at_z(zm))
    stage_d(0)
    z1c.wait_recv()
    stage_a(1)
    z1d.wait_recv()
    stage_a(2)
    stage_e(0)
    stage_f(0)
    stage_b(1)
    stage_b(2)
    stage_c(1)
    stage_c(2)
    stage_d(1)
    stage_d(2)
    z2p.wait_recv()
    z2m.wait_recv()
    stage_a(3)
    row_copies = rows_y(*row_copies)
    stage_e(1)
    stage_e(2)
    stage_f(1)
    stage_f(2)
    stage_g(0)
    stage_b(3)
    stage_c(3)
    stage_d(3)
    stage_g(1)
    stage_g(2)
    stage_e(3)
    stage_f(3)
    last_rows = rows_core()
    stage_g(3)
    finish_rows(last_rows)
    mm_first((0, 1, 2))
    mm_last()

    own_norm = jnp.sum(norm_acc[...], axis=1, keepdims=True)
    plane = (y * 4 + x) * 2 + c
    red_a[plane] = jnp.broadcast_to(own_norm, (1, 128))

    @pl.loop(1, 32)
    def _(k):
        to = lax.rem(plane + k, 32)
        pltpu.make_async_remote_copy(
            src_ref=red_a.at[plane], dst_ref=red_a.at[plane], send_sem=red_send.at[0],
            recv_sem=red_recv.at[0],
            device_id=(to // 8, lax.rem(to // 2, 4), zh, lax.rem(to, 2), zl), device_id_type=MESH,
        ).start()

    pltpu.make_async_copy(red_a.at[pl.ds(0, 31)], red_a.at[pl.ds(0, 31)], red_recv.at[0]).wait()
    z16 = zh * 4 + zl
    red_b[z16] = jnp.sum(red_a[...], axis=0)

    @pl.loop(1, 16)
    def _(k):
        to = lax.rem(z16 + k, 16)
        pltpu.make_async_remote_copy(
            src_ref=red_b.at[z16], dst_ref=red_b.at[z16], send_sem=red_send.at[1],
            recv_sem=red_recv.at[1],
            device_id=(y, x, to // 4, c, lax.rem(to, 4)), device_id_type=MESH,
        ).start()

    for copy in sent:
        copy.wait_send()
    for own, remote in row_copies:

        @pl.when(jnp.logical_not(own))
        def _():
            remote.wait_send()

    pltpu.make_async_copy(red_a.at[pl.ds(0, 31)], red_a.at[pl.ds(0, 31)], red_send.at[0]).wait()
    pltpu.make_async_copy(red_b.at[pl.ds(0, 15)], red_b.at[pl.ds(0, 15)], red_recv.at[1]).wait()
    n_out[...] = jnp.sum(red_b[...], axis=0)
    pltpu.make_async_copy(red_b.at[pl.ds(0, 15)], red_b.at[pl.ds(0, 15)], red_send.at[1]).wait()


def scale_kernel(precond, ratio, norm, p_in, r_in, p_out, r_out, scaled, sem):
    copies = [
        pltpu.make_async_copy(precond.at[0:64], p_in, sem.at[0]),
        pltpu.make_async_copy(precond.at[64:128], p_out, sem.at[1]),
    ]
    for copy in copies:
        copy.start()
    rescale = jnp.sqrt(2.0 * D * H / norm[0:1, 0:1])
    for k, (target, rows) in enumerate(((r_in, 0), (r_in, 32), (r_out, 64), (r_out, 96))):
        scaled[rows : rows + 32] = ratio[rows : rows + 32] * rescale
        copy = pltpu.make_async_copy(
            scaled.at[rows : rows + 32], target.at[pl.ds(rows % 64, 32)], sem.at[2 + k]
        )
        copy.start()
        copies.append(copy)
    for copy in copies:
        copy.wait()


def shards(*args):
    hbm = pl.BlockSpec(memory_space=pltpu.HBM)
    vmem = pl.BlockSpec(memory_space=pltpu.VMEM)
    dma = pltpu.SemaphoreType.DMA
    both = pltpu.VMEM((128, 2048), F32)
    precond, ratio, norm = pl.pallas_call(
        kernel,
        out_shape=(both, both, pltpu.VMEM((1, 128), F32)),
        in_specs=[hbm] * 4,
        out_specs=(vmem,) * 3,
        scratch_shapes=[
            pltpu.VMEM((4, 2048), BF),
            pltpu.VMEM((4, 2048), BF),
            pltpu.VMEM((4, 2048), BF),
            pltpu.VMEM((4, 2048), BF),
            pltpu.VMEM((2, 8, 2048), F32),
            pltpu.VMEM((4, 8, 512), BF),
            pltpu.VMEM((2, 8, 1024), BF),
            pltpu.VMEM((8, 1024), BF),
            pltpu.VMEM((2, 4, 4, 4, 16, 1024), BF),
            pltpu.VMEM((4, 8, 512), BF),
            pltpu.VMEM((4, 4, 8, 128), BF),
            pltpu.VMEM((2, 4, 4, 4, 8, 128), BF),
            pltpu.VMEM((4, 128, 256), BF),
            pltpu.VMEM((4, 128, 256), BF),
            pltpu.VMEM((128, 2048), F32),
            pltpu.VMEM((128, 2048), F32),
            pltpu.VMEM((1, TILE), F32),
            pltpu.VMEM((32, 1, 128), F32),
            pltpu.VMEM((16, 1, 128), F32),
            dma((4,)),
            dma((N_MSG,)),
            dma((N_MSG,)),
            dma((4,)),
            dma((4,)),
            dma((2,)),
            dma((2,)),
            pltpu.SemaphoreType.REGULAR((2,)),
        ],
        compiler_params=pltpu.CompilerParams(
            collective_id=0, has_side_effects=True, vmem_limit_bytes=K1_LIMIT
        ),
    )(*(pltpu.with_memory_space_constraint(v, pltpu.HBM) for v in args))
    half = jax.ShapeDtypeStruct((64, 2048), F32)
    outs = pl.pallas_call(
        scale_kernel,
        out_shape=(half,) * 4,
        in_specs=[vmem] * 3,
        out_specs=(hbm,) * 4,
        scratch_shapes=[pltpu.VMEM((128, 2048), F32), dma((6,))],
        compiler_params=pltpu.CompilerParams(vmem_limit_bytes=8 * 1024 * 1024),
    )(*(pltpu.with_memory_space_constraint(v, pltpu.VMEM) for v in (precond, ratio, norm)))
    return (*outs, norm[0, 0])


def solution(mesh):
    torus = Mesh(mesh.devices.reshape(4, 4, 4, 2, mesh.shape["mp"]), AXES)
    placed = (P(DP, None), P(DP, "mp"), P(DP, "mp"), P(DP, "mp"))
    return jax.shard_map(
        shards,
        mesh=torus,
        in_specs=placed,
        out_specs=(P(DP, "mp"), P(DP, "mp"), P(DP, "mp"), P(DP, "mp"), P()),
        check_vma=False,
    )
```

time: 73.3 us -> 60.7 us (0.83)
  Pallas kernels: 67.6 us -> 58.6 us
  other arithmetic: 2.88 us -> 0 us
    pallas_call x1 -> x2, Pallas kernels: 67.6 us -> 58.6 us  [the longest x1 57.2 us: shards(): pl.pallas_call(kernel, out_shape=(both, both, pltpu.VMEM((1, 128), F32)),...]
    mul x1 -> x0, other arithmetic: 2.88 us -> none  [shards(): ratio[64:] * rescale]
where the time goes in v2:
time: 60.7 us; the launch traced here: 60.4 us
  Pallas kernels  58.6 us (97%)
  between operations  1.81 us (3%)
    pallas_call x1, Pallas kernels, shards(): pl.pallas_call(kernel, out_shape=(both, both, pltpu.VMEM((1, 128), F32)),...  57.2 us
    pallas_call x1, Pallas kernels, shards(): pl.pallas_call(scale_kernel, out_shape=(half,) * 4, in_specs=[vmem] * 3,...  1.36 us

profile of v2, /device:TPU:1, one launch (start us, length us, event | category | flops | bytes accessed | tf_op | source)
XLA Modules:
  0.0 60.4 jit_solution(17441347420361998885)
XLA Ops:
  0.6 57.2 %shard_map.83 = (f32[128,2048]{1,0:T(8,128)S(1)}, f32[128,2048]{1,0:T(8,128)S(1)}, f32[1,128]{1,0:T(1,128)S(1)}) custom-call(bf16[4,8192]{1,0:T(4,128)(2,1)} %li_hbm.1, bf16[4,2048]{1,0:T(4,128)(2,1)} %pre_hbm.1, bf16[4,2048]{1,0:T(4,128)(2,1)} %ha_hbm.1, bf16[4,2048]{1,0:T(4,128)(2,1)} %oa_hbm.1), custom_call_target="tpu_custom_call" | custom-call | tf_op jit(solution)/shard_map/pallas_call | solution.py:398
  57.8 1.4 %shard_map.84 = (f32[64,2048]{1,0:T(8,128)}, f32[64,2048]{1,0:T(8,128)}, f32[64,2048]{1,0:T(8,128)}, f32[64,2048]{1,0:T(8,128)}) custom-call(f32[128,2048]{1,0:T(8,128)S(1)} %get-tuple-element.12.precond, f32[128,2048]{1,0:T(8,128)S(1)} %get-tuple-element.13.ratio, f32[1,128]{1,0:T(1,128)S(1)} %get-tuple-element.14.norm), custom_call_target="tpu_custom_call" | custom-call | tf_op jit(solution)/shard_map/pallas_call | solution.py:437

commit v3 on v2

v3 whole, which is shorter than its diff:
```python
import jax
import jax.numpy as jnp
from jax import lax
from jax.experimental import pallas as pl
from jax.experimental.pallas import tpu as pltpu
from jax.sharding import Mesh
from jax.sharding import PartitionSpec as P

D = 8192
H = 8192
EXAMPLES = 512
DP = ("dp_0", "dp_1", "dp_2", "dp_3")
AXES = ("dp_0", "dp_1", "dp_2", "dp_3", "mp")
MESH = pl.DeviceIdType.MESH
BF = jnp.bfloat16
F32 = jnp.float32

DAMPING = 0.1
EXPONENT = 0.75

SMALL, GATHER, FORWARD, RED_A, RED_B = range(5)
N_LANDED = 52
TILE = 256
K1_LIMIT = 32 * 1024 * 1024


def mod4(a):
    return lax.rem(a, 4)


def kernel(
    li_hbm, pre_hbm, ha_hbm, oa_hbm,
    p_all, r_all, n_out,
    pre_v, ha_v, oa_v, li_v, stack, rows0, pair_src,
    big, rows1, rows2, rows3, lhs_t, lhs_sq, acc_g, acc_s, norm_acc, red_a, red_b,
    in_sem, left, landed, out_sem, hello_sem,
):
    y, x, zh, c, zl = (lax.axis_index(a) for a in AXES)
    d = 1 - c
    f = x * d + y * c
    s = y * d + x * c
    fp, fm, fo = mod4(f + 1), mod4(f + 3), mod4(f + 2)
    sp, sm, so = mod4(s + 1), mod4(s + 3), mod4(s + 2)
    zp, zm, zo = mod4(zh + 1), mod4(zh + 3), mod4(zh + 2)

    def at_f(fd):
        return (y * d + fd * c, fd * d + x * c, zh, c, zl)

    def at_s(sd):
        return (sd * d + y * c, x * d + sd * c, zh, c, zl)

    def at_z(zd, core=None):
        return (y, x, zd, c if core is None else core, zl)

    partner = (y, x, zh, d, zl)

    barrier = pltpu.get_barrier_semaphore()

    def tell(semaphore, device):
        pl.semaphore_signal(semaphore, inc=1, device_id=device, device_id_type=MESH)

    for core in (c, d):
        tell(barrier, at_z(zp, core))
        tell(barrier, at_z(zm, core))
    for k in (1, 2, 3):
        tell(barrier, (y, x, zh, c, mod4(zl + k)))
        tell(barrier, (mod4(y + k), x, zh, c, zl))
        tell(barrier, (y, mod4(x + k), zh, c, zl))
    tell(barrier, partner)

    loads = [
        pltpu.make_async_copy(pre_hbm, pre_v, in_sem.at[0]),
        pltpu.make_async_copy(ha_hbm, ha_v, in_sem.at[1]),
        pltpu.make_async_copy(oa_hbm, oa_v, in_sem.at[2]),
        pltpu.make_async_copy(
            li_hbm.at[:, pl.ds(pl.multiple_of(zl * 2048, 2048), 2048)], li_v, in_sem.at[3]
        ),
    ]
    for load in loads:
        load.start()
    for load in loads:
        load.wait()
    preact = pre_v[...].astype(F32)
    logistic = 1.0 / (1.0 + jnp.exp(-preact))
    hidden = (preact * logistic).astype(BF)
    adjoint = (ha_v[...].astype(F32) * logistic * (1.0 + preact * (1.0 - logistic))).astype(BF)
    stack[0, 0:4, :] = adjoint.astype(F32)
    stack[0, 4:8, :] = oa_v[...].astype(F32)
    stack[1, 0:4, :] = li_v[...].astype(F32)
    stack[1, 4:8, :] = hidden.astype(F32)
    pair_src[0] = stack[0, :, 0:1024].astype(BF)
    pair_src[1] = stack[0, :, 1024:2048].astype(BF)
    big[c, zh, y, x, c] = pair_src[c]
    for k in range(4):
        rows0[k] = stack[1, :, 512 * k : 512 * (k + 1)].astype(BF)

    pl.semaphore_wait(barrier, 14)

    places = {}

    def place(key):
        return landed.at[places.setdefault(key, len(places))]

    def send(src, dst, device, key, group):
        pltpu.make_async_remote_copy(
            src_ref=src, dst_ref=dst, send_sem=left.at[group], recv_sem=place(key),
            device_id=device, device_id_type=MESH,
        ).start()

    def take(ref, semaphore):
        pltpu.make_async_copy(ref, ref, semaphore).wait()

    def arrived(ref, key):
        take(ref, place(key))

    one = big.at[0, 0, 0, 0]
    half_block = big.at[0, 0, 0, 0, :, :, 0:512]

    def block(z, sd, fd):
        return big.at[c, z, sd * d + fd * c, fd * d + sd * c]

    def half(z, sd, fd, k):
        return big.at[c, z, sd * d + fd * c, fd * d + sd * c, :, :, pl.ds(512 * k, 512)]

    def z_pieces(zd, k, key):
        cols = pl.ds(512 * k, 512)
        for core in (c, d):
            send(
                pair_src.at[core, :, cols], big.at[core, zh, y, x, c, :, cols],
                at_z(zd, core), key, SMALL,
            )

    z_pieces(zp, 0, "z1a")
    z_pieces(zm, 1, "z1b")
    send(pair_src.at[d], big.at[d, zh, y, x, c], partner, "pair", SMALL)
    for k in (1, 2, 3):
        xd = mod4(x + k)
        send(rows0.at[xd], rows1.at[x], (y, xd, zh, c, zl), "row_x", SMALL)
    row_own = pltpu.make_async_copy(rows0.at[x], rows1.at[x], in_sem.at[0])
    row_own.start()
    z_pieces(zp, 1, "z1c")
    z_pieces(zm, 0, "z1d")
    tell(hello_sem.at[0], at_z(zp))
    for k in (1, 2, 3):
        tell(hello_sem.at[1], (mod4(y + k), x, zh, c, zl))

    def rows_z():
        arrived(rows1.at[0:3], "row_x")
        row_own.wait()
        pl.semaphore_wait(hello_sem.at[0], 1)
        for zd, key in ((zo, "row_z_far"), (zp, "row_z"), (zm, "row_z")):
            cols = pl.ds(pl.multiple_of(zd * 128, 128), 128)
            send(rows1.at[:, :, cols], rows2.at[zh], at_z(zd), key, SMALL)
        local = pltpu.make_async_copy(
            rows1.at[:, :, pl.ds(pl.multiple_of(zh * 128, 128), 128)], rows2.at[zh], in_sem.at[1]
        )
        local.start()
        return local

    def rows_y(planes, key):
        for zd in range(4):
            own = jnp.logical_and(y == zl, zl == zd)
            for z in planes:

                @pl.when(own)
                def _():
                    pltpu.make_async_copy(rows2.at[z], rows3.at[c, z, y], place(key)).start()

                @pl.when(jnp.logical_not(own))
                def _():
                    pltpu.make_async_remote_copy(
                        src_ref=rows2.at[z], dst_ref=rows3.at[c, z, y], send_sem=out_sem.at[zd],
                        recv_sem=place(key), device_id=(zl, x, zh, c, zd), device_id_type=MESH,
                    ).start()

    def rows_near(local):
        arrived(rows2.at[0:2], "row_z")
        local.wait()
        pl.semaphore_wait(hello_sem.at[1], 3)
        rows_y((zh, zm, zp), "row_y")

    def rows_far():
        arrived(rows2.at[0], "row_z_far")
        rows_y((zo,), "row_y_far")

    def rows_core_near():
        arrived(rows3.at[0, 0:3], "row_y")
        for z in (zh, zm, zp):
            send(rows3.at[c, z], rows3.at[c, z], partner, "row_core", SMALL)

    def rows_core_far():
        arrived(rows3.at[0, 0], "row_y_far")
        send(rows3.at[c, zo], rows3.at[c, zo], partner, "row_core_far", SMALL)

    slices = (zh, zm, zp, zo)
    routes = {0: "++--", 1: "++--", 2: "++--", 3: "-+-*"}

    def s_key(k, j, side):
        relayed = {"+": 0, "-": 1}.get(routes[k][j])
        if relayed == side:
            return ("s1", k, j)
        return ("rest", k, 0)

    def far_key(k):
        return ("rest", k, 1 if k == 3 else 0)

    def both_s(k, j, fd):
        z = slices[k]
        send(block(z, s, fd), block(z, s, fd), at_s(sp), s_key(k, j, 0), GATHER)
        send(block(z, s, fd), block(z, s, fd), at_s(sm), s_key(k, j, 1), GATHER)
        if routes[k][j] == "*":
            send(block(z, s, fd), block(z, s, fd), at_s(so), far_key(k), GATHER)

    def relay(k, j, fd):
        z = slices[k]
        arrived(one, ("s1", k, j))
        came, goes = (sm, sp) if routes[k][j] == "+" else (sp, sm)
        send(block(z, came, fd), block(z, came, fd), at_s(goes), far_key(k), GATHER)

    def stage_a(k):
        z = slices[k]
        send(block(z, s, f), block(z, s, f), at_f(fp), ("f1", k, 0), GATHER)
        send(block(z, s, f), block(z, s, f), at_f(fm), ("f1", k, 1), GATHER)
        both_s(k, 0, f)
        send(block(z, s, f), block(z, s, f), at_f(fo), ("f2", k), GATHER)

    def stage_b(k):
        arrived(one, ("f1", k, 0))
        both_s(k, 1, fm)
        arrived(one, ("f1", k, 1))
        both_s(k, 2, fp)

    def stage_c(k):
        relay(k, 0, f)

    def stage_d(k):
        arrived(one, ("f2", k))
        both_s(k, 3, fo)

    def stage_e(k):
        relay(k, 1, fm)
        relay(k, 2, fp)

    def stage_f(k):
        relay(k, 3, fo)

    def stage_g(k):
        z = slices[k]
        arrived(big.at[0, 0, 0:2], ("rest", k, 0))
        send(big.at[c, z], big.at[c, z], partner, ("x", k), FORWARD)

    def forward(z, sd):
        for fd in (f, fm, fp, fo):
            send(block(z, sd, fd), block(z, sd, fd), partner, ("x", 3), FORWARD)

    def last_near():
        arrived(big.at[0, 0, 0:2, :, :, :, 0:640], ("rest", 3, 0))
        forward(zo, sm)
        forward(zo, sp)

    def last_far():
        arrived(big.at[0, 0, 0], ("rest", 3, 1))
        forward(zo, so)

    def finish_rows(z):
        row = lax.broadcasted_iota(jnp.int32, (256, 128), 0)
        lane = lax.broadcasted_iota(jnp.int32, (256, 128), 1)
        keep = lax.rem(row // 4, 2) == lane // 64
        straight = lane // 64 == c
        parts = [rows3[core, z].reshape(16, 8, 128).astype(F32) for core in range(2)]
        data = jnp.stack(parts, axis=1).reshape(256, 128)
        turned = pltpu.roll(data, 64, 1)
        t = jnp.transpose(jnp.where(keep, jnp.where(straight, data, turned), 0.0))
        lhs_t[z] = t.astype(BF)
        lhs_sq[z] = (t * t).astype(BF)

    def finish_near():
        arrived(rows3.at[0, 0:3], "row_core")

        @pl.loop(0, 3)
        def _(k):
            finish_rows(mod4(zh + k + 3))

    def finish_far():
        arrived(rows3.at[0, 0], "row_core_far")
        finish_rows(zo)

    def dots(zs, j):
        cols = pl.ds(pl.multiple_of(lax.rem(j, 4) * TILE, TILE), TILE)
        rights = [big[j // 4, z, :, :, :, :, cols].astype(F32).reshape(256, TILE) for z in zs]
        right = jnp.concatenate(rights, axis=0)
        left_t = jnp.concatenate([lhs_t[z] for z in zs], axis=1)
        left_sq = jnp.concatenate([lhs_sq[z] for z in zs], axis=1)
        grad = jnp.dot(left_t, right.astype(BF), preferred_element_type=F32)
        square = jnp.dot(left_sq, (right * right).astype(BF), preferred_element_type=F32)
        return grad, square

    def mm_part(ks, first):
        for k in ks:
            arrived(big.at[0, 0], ("x", k))

        @pl.loop(0, 8, unroll=8)
        def _(j):
            grad, square = dots([slices[k] for k in ks], j)
            wide = pl.ds(pl.multiple_of(j * TILE, TILE), TILE)
            if first:
                acc_g[:, wide] = grad
                acc_s[:, wide] = square
            else:
                acc_g[:, wide] += grad
                acc_s[:, wide] += square

    def mm_last():
        arrived(big.at[0, 0], ("x", 3))
        norm_acc[...] = jnp.zeros_like(norm_acc)

        @pl.loop(0, 8, unroll=8)
        def _(j):
            grad, square = dots([zo], j)
            wide = pl.ds(pl.multiple_of(j * TILE, TILE), TILE)
            grad = (acc_g[:, wide] + grad) * (1.0 / EXAMPLES)
            base = (acc_s[:, wide] + square) * (1.0 / EXAMPLES) + DAMPING
            power = EXPONENT * jnp.log(base)
            ratio = grad * jnp.exp(-power)
            p_all[:, wide] = jnp.exp(power)
            r_all[:, wide] = ratio
            norm_acc[...] += jnp.sum((grad * ratio).reshape(16, 8, TILE), axis=0)

    arrived(big.at[0, 0, 0, 0, 0], "pair")
    stage_a(0)
    stage_b(0)
    stage_c(0)
    rows_own = rows_z()
    stage_d(0)
    arrived(half_block, "z1a")
    send(half(zm, s, f, 0), half(zm, s, f, 0), at_z(zp), "z2p", SMALL)
    arrived(half_block, "z1b")
    send(half(zp, s, f, 1), half(zp, s, f, 1), at_z(zm), "z2m", SMALL)
    arrived(half_block, "z1c")
    stage_a(1)
    arrived(half_block, "z1d")
    stage_a(2)
    stage_e(0)
    stage_f(0)
    stage_b(1)
    stage_b(2)
    stage_c(1)
    stage_c(2)
    stage_d(1)
    stage_d(2)
    rows_near(rows_own)
    arrived(half_block, "z2p")
    arrived(half_block, "z2m")
    stage_a(3)
    stage_e(1)
    stage_e(2)
    stage_g(0)
    stage_f(1)
    stage_f(2)
    stage_b(3)
    stage_c(3)
    rows_far()
    stage_d(3)
    rows_core_near()
    stage_g(1)
    stage_g(2)
    stage_e(3)
    forward(zo, s)
    rows_core_far()
    finish_near()
    mm_part((0, 1, 2), True)
    last_near()
    last_far()
    finish_far()
    mm_last()

    own_norm = jnp.sum(jnp.sum(norm_acc[...], axis=1, keepdims=True), axis=0, keepdims=True)
    plane = (y * 4 + x) * 2 + c
    red_a[plane] = jnp.broadcast_to(own_norm, (1, 128))

    @pl.loop(0, 31)
    def _(k):
        to = lax.rem(plane + 1 + lax.rem(k + 16, 31), 32)
        send(
            red_a.at[plane], red_a.at[plane],
            (to // 8, lax.rem(to // 2, 4), zh, lax.rem(to, 2), zl), "red_a", RED_A,
        )

    arrived(red_a.at[0:31], "red_a")
    z16 = zh * 4 + zl
    red_b[z16] = jnp.sum(red_a[...], axis=0)

    @pl.loop(0, 15)
    def _(k):
        to = lax.rem(z16 + 1 + lax.rem(k + 7, 15), 16)
        send(
            red_b.at[z16], red_b.at[z16], (y, x, to // 4, c, lax.rem(to, 4)), "red_b", RED_B
        )

    take(big.at[:, 0:3, 0:3, 0, 0], left.at[SMALL])
    take(big.at[:, 0:3, :, :, :, :, 0:640], left.at[GATHER])
    take(big.at[0], left.at[FORWARD])
    for zd in range(4):

        @pl.when(jnp.logical_not(jnp.logical_and(y == zl, zl == zd)))
        def _():
            take(rows2, out_sem.at[zd])

    take(red_a.at[0:31], left.at[RED_A])
    arrived(red_b.at[0:15], "red_b")
    n_out[...] = jnp.sum(red_b[...], axis=0)
    take(red_b.at[0:15], left.at[RED_B])
    assert len(places) == N_LANDED, len(places)


def scale_kernel(precond, ratio, norm, p_in, r_in, p_out, r_out, scaled, sem):
    copies = [
        pltpu.make_async_copy(precond.at[0:64], p_in, sem.at[0]),
        pltpu.make_async_copy(precond.at[64:128], p_out, sem.at[1]),
    ]
    for copy in copies:
        copy.start()
    rescale = jnp.sqrt(2.0 * D * H / norm[0:1, 0:1])
    for k, (target, rows) in enumerate(((r_in, 0), (r_in, 32), (r_out, 64), (r_out, 96))):
        scaled[rows : rows + 32] = ratio[rows : rows + 32] * rescale
        copy = pltpu.make_async_copy(
            scaled.at[rows : rows + 32], target.at[pl.ds(rows % 64, 32)], sem.at[2 + k]
        )
        copy.start()
        copies.append(copy)
    for copy in copies:
        copy.wait()


def shards(*args):
    hbm = pl.BlockSpec(memory_space=pltpu.HBM)
    vmem = pl.BlockSpec(memory_space=pltpu.VMEM)
    dma = pltpu.SemaphoreType.DMA
    both = pltpu.VMEM((128, 2048), F32)
    precond, ratio, norm = pl.pallas_call(
        kernel,
        out_shape=(both, both, pltpu.VMEM((1, 128), F32)),
        in_specs=[hbm] * 4,
        out_specs=(vmem,) * 3,
        scratch_shapes=[
            pltpu.VMEM((4, 2048), BF),
            pltpu.VMEM((4, 2048), BF),
            pltpu.VMEM((4, 2048), BF),
            pltpu.VMEM((4, 2048), BF),
            pltpu.VMEM((2, 8, 2048), F32),
            pltpu.VMEM((4, 8, 512), BF),
            pltpu.VMEM((2, 8, 1024), BF),
            pltpu.VMEM((2, 4, 4, 4, 2, 8, 1024), BF),
            pltpu.VMEM((4, 8, 512), BF),
            pltpu.VMEM((4, 4, 8, 128), BF),
            pltpu.VMEM((2, 4, 4, 4, 8, 128), BF),
            pltpu.VMEM((4, 128, 256), BF),
            pltpu.VMEM((4, 128, 256), BF),
            pltpu.VMEM((128, 2048), F32),
            pltpu.VMEM((128, 2048), F32),
            pltpu.VMEM((8, TILE), F32),
            pltpu.VMEM((32, 1, 128), F32),
            pltpu.VMEM((16, 1, 128), F32),
            dma((4,)),
            dma((5,)),
            dma((N_LANDED,)),
            dma((4,)),
            pltpu.SemaphoreType.REGULAR((2,)),
        ],
        compiler_params=pltpu.CompilerParams(
            collective_id=0, has_side_effects=True, vmem_limit_bytes=K1_LIMIT
        ),
    )(*(pltpu.with_memory_space_constraint(v, pltpu.HBM) for v in args))
    half = jax.ShapeDtypeStruct((64, 2048), F32)
    outs = pl.pallas_call(
        scale_kernel,
        out_shape=(half,) * 4,
        in_specs=[vmem] * 3,
        out_specs=(hbm,) * 4,
        scratch_shapes=[pltpu.VMEM((128, 2048), F32), dma((6,))],
        compiler_params=pltpu.CompilerParams(vmem_limit_bytes=8 * 1024 * 1024),
    )(*(pltpu.with_memory_space_constraint(v, pltpu.VMEM) for v in (precond, ratio, norm)))
    return (*outs, norm[0, 0])


def solution(mesh):
    torus = Mesh(mesh.devices.reshape(4, 4, 4, 2, mesh.shape["mp"]), AXES)
    placed = (P(DP, None), P(DP, "mp"), P(DP, "mp"), P(DP, "mp"))
    return jax.shard_map(
        shards,
        mesh=torus,
        in_specs=placed,
        out_specs=(P(DP, "mp"), P(DP, "mp"), P(DP, "mp"), P(DP, "mp"), P()),
        check_vma=False,
    )
```

time: 60.7 us -> 55.2 us (0.909)
  Pallas kernels: 58.6 us -> 53 us
    pallas_call x1, Pallas kernels: 57.2 us -> 51.7 us  [shards(): pl.pallas_call(kernel, out_shape=(both, both, pltpu.VMEM((1, 128), F32)),...]
where the time goes in v3:
time: 55.2 us; the launch traced here: 54.8 us
  Pallas kernels  53 us (96%)
  between operations  1.81 us (3%)
    pallas_call x1, Pallas kernels, shards(): pl.pallas_call(kernel, out_shape=(both, both, pltpu.VMEM((1, 128), F32)),...  51.7 us
    pallas_call x1, Pallas kernels, shards(): pl.pallas_call(scale_kernel, out_shape=(half,) * 4, in_specs=[vmem] * 3,...  1.36 us

profile of v3, /device:TPU:1, one launch (start us, length us, event | category | flops | bytes accessed | tf_op | source)
XLA Modules:
  0.0 54.8 jit_solution(1594681549639040861)
XLA Ops:
  0.6 51.7 %shard_map.83 = (f32[128,2048]{1,0:T(8,128)S(1)}, f32[128,2048]{1,0:T(8,128)S(1)}, f32[1,128]{1,0:T(1,128)S(1)}) custom-call(bf16[4,8192]{1,0:T(4,128)(2,1)} %li_hbm.1, bf16[4,2048]{1,0:T(4,128)(2,1)} %pre_hbm.1, bf16[4,2048]{1,0:T(4,128)(2,1)} %ha_hbm.1, bf16[4,2048]{1,0:T(4,128)(2,1)} %oa_hbm.1), custom_call_target="tpu_custom_call" | custom-call | tf_op jit(solution)/shard_map/pallas_call | solution.py:440
  52.3 1.4 %shard_map.84 = (f32[64,2048]{1,0:T(8,128)}, f32[64,2048]{1,0:T(8,128)}, f32[64,2048]{1,0:T(8,128)}, f32[64,2048]{1,0:T(8,128)}) custom-call(f32[128,2048]{1,0:T(8,128)S(1)} %get-tuple-element.12.precond, f32[128,2048]{1,0:T(8,128)S(1)} %get-tuple-element.13.ratio, f32[1,128]{1,0:T(1,128)S(1)} %get-tuple-element.14.norm), custom_call_target="tpu_custom_call" | custom-call | tf_op jit(solution)/shard_map/pallas_call | solution.py:475

commit v4 on v3

--- a/solution.py
+++ b/solution.py
@@ -204,18 +204,24 @@
     def far_key(k):
         return ("rest", k, 1 if k == 3 else 0)
 
+    def forward(k, sd, fd):
+        z = slices[k]
+        send(block(z, sd, fd), block(z, sd, fd), partner, ("x", k), FORWARD)
+
     def both_s(k, j, fd):
         z = slices[k]
         send(block(z, s, fd), block(z, s, fd), at_s(sp), s_key(k, j, 0), GATHER)
         send(block(z, s, fd), block(z, s, fd), at_s(sm), s_key(k, j, 1), GATHER)
         if routes[k][j] == "*":
             send(block(z, s, fd), block(z, s, fd), at_s(so), far_key(k), GATHER)
+        forward(k, s, fd)
 
     def relay(k, j, fd):
         z = slices[k]
         arrived(one, ("s1", k, j))
         came, goes = (sm, sp) if routes[k][j] == "+" else (sp, sm)
         send(block(z, came, fd), block(z, came, fd), at_s(goes), far_key(k), GATHER)
+        forward(k, came, fd)
 
     def stage_a(k):
         z = slices[k]
@@ -244,23 +250,27 @@
     def stage_f(k):
         relay(k, 3, fo)
 
+    def forward_near(k):
+        for j, fd in enumerate((f, fm, fp, fo)):
+            if routes[k][j] != "+":
+                forward(k, sm, fd)
+            if routes[k][j] != "-":
+                forward(k, sp, fd)
+
     def stage_g(k):
-        z = slices[k]
         arrived(big.at[0, 0, 0:2], ("rest", k, 0))
-        send(big.at[c, z], big.at[c, z], partner, ("x", k), FORWARD)
-
-    def forward(z, sd):
+        forward_near(k)
         for fd in (f, fm, fp, fo):
-            send(block(z, sd, fd), block(z, sd, fd), partner, ("x", 3), FORWARD)
+            forward(k, so, fd)
 
     def last_near():
         arrived(big.at[0, 0, 0:2, :, :, :, 0:640], ("rest", 3, 0))
-        forward(zo, sm)
-        forward(zo, sp)
+        forward_near(3)
 
     def last_far():
         arrived(big.at[0, 0, 0], ("rest", 3, 1))
-        forward(zo, so)
+        for fd in (f, fm, fp, fo):
+            forward(3, so, fd)
 
     def finish_rows(z):
         row = lax.broadcasted_iota(jnp.int32, (256, 128), 0)
@@ -365,7 +375,6 @@
     stage_g(1)
     stage_g(2)
     stage_e(3)
-    forward(zo, s)
     rows_core_far()
     finish_near()
     mm_part((0, 1, 2), True)
@@ -378,7 +387,7 @@
     plane = (y * 4 + x) * 2 + c
     red_a[plane] = jnp.broadcast_to(own_norm, (1, 128))
 
-    @pl.loop(0, 31)
+    @pl.loop(0, 31, unroll=31)
     def _(k):
         to = lax.rem(plane + 1 + lax.rem(k + 16, 31), 32)
         send(
@@ -390,7 +399,7 @@
     z16 = zh * 4 + zl
     red_b[z16] = jnp.sum(red_a[...], axis=0)
 
-    @pl.loop(0, 15)
+    @pl.loop(0, 15, unroll=15)
     def _(k):
         to = lax.rem(z16 + 1 + lax.rem(k + 7, 15), 16)
         send(
@@ -413,10 +422,11 @@
     assert len(places) == N_LANDED, len(places)
 
 
-def scale_kernel(precond, ratio, norm, p_in, r_in, p_out, r_out, scaled, sem):
+def scale_kernel(precond, ratio, norm, p_in, r_in, p_out, r_out, n_out, scaled, sem):
     copies = [
         pltpu.make_async_copy(precond.at[0:64], p_in, sem.at[0]),
         pltpu.make_async_copy(precond.at[64:128], p_out, sem.at[1]),
+        pltpu.make_async_copy(norm, n_out, sem.at[6]),
     ]
     for copy in copies:
         copy.start()
@@ -472,12 +482,12 @@
         ),
     )(*(pltpu.with_memory_space_constraint(v, pltpu.HBM) for v in args))
     half = jax.ShapeDtypeStruct((64, 2048), F32)
-    outs = pl.pallas_call(
+    *outs, norm = pl.pallas_call(
         scale_kernel,
-        out_shape=(half,) * 4,
+        out_shape=(half, half, half, half, jax.ShapeDtypeStruct((1, 128), F32)),
         in_specs=[vmem] * 3,
-        out_specs=(hbm,) * 4,
-        scratch_shapes=[pltpu.VMEM((128, 2048), F32), dma((6,))],
+        out_specs=(hbm,) * 5,
+        scratch_shapes=[pltpu.VMEM((128, 2048), F32), dma((7,))],
         compiler_params=pltpu.CompilerParams(vmem_limit_bytes=8 * 1024 * 1024),
     )(*(pltpu.with_memory_space_constraint(v, pltpu.VMEM) for v in (precond, ratio, norm)))
     return (*outs, norm[0, 0])

time: 55.2 us -> 53.2 us (0.964)
  between operations: 1.81 us -> 0.64 us
  Pallas kernels: 53 us -> 52.4 us
    pallas_call x1, Pallas kernels: 51.7 us -> 51 us  [shards(): pl.pallas_call(kernel, out_shape=(both, both, pltpu.VMEM((1, 128), F32)),...]
where the time goes in v4:
time: 53.2 us; the launch traced here: 53 us
  Pallas kernels  52.4 us (98%)
  between operations  0.64 us (1%)
    pallas_call x1, Pallas kernels, shards(): pl.pallas_call(kernel, out_shape=(both, both, pltpu.VMEM((1, 128), F32)),...  51 us
    pallas_call x1, Pallas kernels, shards(): pl.pallas_call(scale_kernel, out_shape=(half, half, half, half, jax.Shape...  1.37 us

profile of v4, /device:TPU:1, one launch (start us, length us, event | category | flops | bytes accessed | tf_op | source)
XLA Modules:
  0.0 53.0 jit_solution(12141877684667917399)
XLA Ops:
  0.6 51.0 %shard_map.83 = (f32[128,2048]{1,0:T(8,128)S(1)}, f32[128,2048]{1,0:T(8,128)S(1)}, f32[1,128]{1,0:T(1,128)S(1)}) custom-call(bf16[4,8192]{1,0:T(4,128)(2,1)} %li_hbm.1, bf16[4,2048]{1,0:T(4,128)(2,1)} %pre_hbm.1, bf16[4,2048]{1,0:T(4,128)(2,1)} %ha_hbm.1, bf16[4,2048]{1,0:T(4,128)(2,1)} %oa_hbm.1), custom_call_target="tpu_custom_call" | custom-call | tf_op jit(solution)/shard_map/pallas_call | solution.py:450
  51.6 1.4 %shard_map.84 = (f32[64,2048]{1,0:T(8,128)}, f32[64,2048]{1,0:T(8,128)}, f32[64,2048]{1,0:T(8,128)}, f32[64,2048]{1,0:T(8,128)}, f32[1,128]{1,0:T(1,128)}) custom-call(f32[128,2048]{1,0:T(8,128)S(1)} %get-tuple-element.13.precond, f32[128,2048]{1,0:T(8,128)S(1)} %get-tuple-element.14.ratio, f32[1,128]{1,0:T(1,128)S(1)} %get-tuple-element.15.norm), custom_call_target="tpu_custom_call" | custom-call | tf_op jit(solution)/shard_map/pallas_call | solution.py:485

commit v5 on v4

--- a/solution.py
+++ b/solution.py
@@ -19,7 +19,7 @@
 EXPONENT = 0.75
 
 SMALL, GATHER, FORWARD, RED_A, RED_B = range(5)
-N_LANDED = 52
+N_LANDED = 49
 TILE = 256
 K1_LIMIT = 32 * 1024 * 1024
 
@@ -193,7 +193,7 @@
         send(rows3.at[c, zo], rows3.at[c, zo], partner, "row_core_far", SMALL)
 
     slices = (zh, zm, zp, zo)
-    routes = {0: "++--", 1: "++--", 2: "++--", 3: "-+-*"}
+    routes = {0: "++--", 1: "++--", 2: "++--", 3: "****"}
 
     def s_key(k, j, side):
         relayed = {"+": 0, "-": 1}.get(routes[k][j])
@@ -217,6 +217,8 @@
         forward(k, s, fd)
 
     def relay(k, j, fd):
+        if routes[k][j] == "*":
+            return
         z = slices[k]
         arrived(one, ("s1", k, j))
         came, goes = (sm, sp) if routes[k][j] == "+" else (sp, sm)
@@ -264,7 +266,7 @@
             forward(k, so, fd)
 
     def last_near():
-        arrived(big.at[0, 0, 0:2, :, :, :, 0:640], ("rest", 3, 0))
+        arrived(big.at[0, 0, 0:2], ("rest", 3, 0))
         forward_near(3)
 
     def last_far():
@@ -377,9 +379,9 @@
     stage_e(3)
     rows_core_far()
     finish_near()
-    mm_part((0, 1, 2), True)
     last_near()
     last_far()
+    mm_part((0, 1, 2), True)
     finish_far()
     mm_last()
 

time: 53.2 us -> 52.5 us (0.987)
  Pallas kernels: 52.4 us -> 51.7 us
    pallas_call x1, Pallas kernels: 51 us -> 50.3 us  [shards(): pl.pallas_call(kernel, out_shape=(both, both, pltpu.VMEM((1, 128), F32)),...]
where the time goes in v5:
time: 52.5 us; the launch traced here: 52.3 us
  Pallas kernels  51.7 us (98%)
  between operations  0.64 us (1%)
    pallas_call x1, Pallas kernels, shards(): pl.pallas_call(kernel, out_shape=(both, both, pltpu.VMEM((1, 128), F32)),...  50.3 us
    pallas_call x1, Pallas kernels, shards(): pl.pallas_call(scale_kernel, out_shape=(half, half, half, half, jax.Shape...  1.37 us

profile of v5, /device:TPU:1, one launch (start us, length us, event | category | flops | bytes accessed | tf_op | source)
XLA Modules:
  0.0 52.3 jit_solution(5672719364185830009)
XLA Ops:
  0.6 50.3 %shard_map.83 = (f32[128,2048]{1,0:T(8,128)S(1)}, f32[128,2048]{1,0:T(8,128)S(1)}, f32[1,128]{1,0:T(1,128)S(1)}) custom-call(bf16[4,8192]{1,0:T(4,128)(2,1)} %li_hbm.1, bf16[4,2048]{1,0:T(4,128)(2,1)} %pre_hbm.1, bf16[4,2048]{1,0:T(4,128)(2,1)} %ha_hbm.1, bf16[4,2048]{1,0:T(4,128)(2,1)} %oa_hbm.1), custom_call_target="tpu_custom_call" | custom-call | tf_op jit(solution)/shard_map/pallas_call | solution.py:452
  51.0 1.4 %shard_map.84 = (f32[64,2048]{1,0:T(8,128)}, f32[64,2048]{1,0:T(8,128)}, f32[64,2048]{1,0:T(8,128)}, f32[64,2048]{1,0:T(8,128)}, f32[1,128]{1,0:T(1,128)}) custom-call(f32[128,2048]{1,0:T(8,128)S(1)} %get-tuple-element.13.precond, f32[128,2048]{1,0:T(8,128)S(1)} %get-tuple-element.14.ratio, f32[1,128]{1,0:T(1,128)S(1)} %get-tuple-element.15.norm), custom_call_target="tpu_custom_call" | custom-call | tf_op jit(solution)/shard_map/pallas_call | solution.py:487

commit v6 on v5

--- a/solution.py
+++ b/solution.py
@@ -367,9 +367,18 @@
     stage_e(1)
     stage_e(2)
     stage_g(0)
-    stage_f(1)
-    stage_f(2)
-    stage_b(3)
+    @pl.when(c == 0)
+    def _():
+        stage_b(3)
+        stage_f(1)
+        stage_f(2)
+
+    @pl.when(c == 1)
+    def _():
+        stage_f(1)
+        stage_f(2)
+        stage_b(3)
+
     stage_c(3)
     rows_far()
     stage_d(3)

time: 52.5 us -> 52.2 us (level)
  no operation moved by 1% of the time
where the time goes in v6:
time: 52.2 us; the launch traced here: 52 us
  Pallas kernels  51.3 us (98%)
  between operations  0.64 us (1%)
    pallas_call x1, Pallas kernels, shards(): pl.pallas_call(kernel, out_shape=(both, both, pltpu.VMEM((1, 128), F32)),...  50 us
    pallas_call x1, Pallas kernels, shards(): pl.pallas_call(scale_kernel, out_shape=(half, half, half, half, jax.Shape...  1.37 us

profile of v6, /device:TPU:1, one launch (start us, length us, event | category | flops | bytes accessed | tf_op | source)
XLA Modules:
  0.0 52.0 jit_solution(776041339374488870)
XLA Ops:
  0.6 50.0 %shard_map.83 = (f32[128,2048]{1,0:T(8,128)S(1)}, f32[128,2048]{1,0:T(8,128)S(1)}, f32[1,128]{1,0:T(1,128)S(1)}) custom-call(bf16[4,8192]{1,0:T(4,128)(2,1)} %li_hbm.1, bf16[4,2048]{1,0:T(4,128)(2,1)} %pre_hbm.1, bf16[4,2048]{1,0:T(4,128)(2,1)} %ha_hbm.1, bf16[4,2048]{1,0:T(4,128)(2,1)} %oa_hbm.1), custom_call_target="tpu_custom_call" | custom-call | tf_op jit(solution)/shard_map/pallas_call | solution.py:461
  50.6 1.4 %shard_map.84 = (f32[64,2048]{1,0:T(8,128)}, f32[64,2048]{1,0:T(8,128)}, f32[64,2048]{1,0:T(8,128)}, f32[64,2048]{1,0:T(8,128)}, f32[1,128]{1,0:T(1,128)}) custom-call(f32[128,2048]{1,0:T(8,128)S(1)} %get-tuple-element.13.precond, f32[128,2048]{1,0:T(8,128)S(1)} %get-tuple-element.14.ratio, f32[1,128]{1,0:T(1,128)S(1)} %get-tuple-element.15.norm), custom_call_target="tpu_custom_call" | custom-call | tf_op jit(solution)/shard_map/pallas_call | solution.py:496
